TPU v7x, 32 devices: a whole 2x2x4 slice. The times are simulated.
32 devices in a mesh: replica: 2 (over x), tp: 8 (over z, y), sub: 2 (over core).
Axes of the slice: x: 2, y: 2, z: 4, core: 2. Of those that a mesh axis runs over, the one named last changes fastest.
Arguments:
- hidden_in: bfloat16 [8, 8192], P('replica'), parts along dimension 0, may hold values from -6 to 6
- norm_gain: float32 [16384], P('replica'), parts along dimension 0, may hold values from 0.1 to 1.9
- wqkv_old: bfloat16 [16, 2, 1280, 4096], P(('replica', 'tp'), 'sub'), parts along dimension 0, may hold values from -0.1875 to 0.1875
- wo: bfloat16 [16384, 8192], P(('replica', 'tp', 'sub')), parts along dimension 0, may hold values from -0.0625 to 0.0625
- key_cache: bfloat16 [8, 4096, 1024], P('replica', ('tp', 'sub')), parts along dimension 0, may hold values from -240 to 240
- value_cache: bfloat16 [8, 4096, 1024], P('replica', ('tp', 'sub')), parts along dimension 0, may hold values from -6 to 6
- lengths: int32 [8], P('replica'), parts along dimension 0, may hold values from 1 to 4096
- section_order: int32 [32], P('replica'), parts along dimension 0, may hold values from 0 to 15, each once
Outputs:
- mixed_out: bfloat16 [8, 8192], P('replica'), parts along dimension 0
- wqkv_new: bfloat16 [16, 2, 640, 8192], P(('replica', 'tp'), 'sub'), parts along dimension 0
There are 2 independent parts, one for each index of `replica`. A program takes and returns all parts, laid end to end along the dimension named above; each array names one. Nothing has to cross between parts.
Inputs may be any that keep to these rules, and one draw needn't show every extreme that they name: `section_order`: each input row block appears once. The new token's position is lengths[b].
All inputs are finite; a program needn't handle non-finite values.
Results may differ from a plain program's by a relative error of at most 0.0085.
The roundings to bfloat16 on the way count: a program that leaves them out, or rounds other values in their place, can miss the bound.
Values may be sent and summed in bfloat16 or wider, within the bound.
A program may use at most 128 MiB of HBM per device.

v0:
```python
import math
import jax
import jax.numpy as jnp
from jax import lax
from jax.sharding import PartitionSpec as P

HEADS = 64
KV_HEADS = 8
HEAD_DIM = 128
RANKS = 8
ROW_BLOCKS = 16


def passed_along(value, axis, steps):
    count = lax.axis_size(axis)
    pairs = [(source, (source + steps) % count) for source in range(count)]
    return lax.ppermute(value, axis, pairs)


def rotary(values, positions):
    half = values.shape[-1] // 2
    freqs = 500000.0 ** (-jnp.arange(half, dtype=jnp.float32) * 2.0 / values.shape[-1])
    angles = positions.astype(jnp.float32)[:, None] * freqs[None, :]
    cosine = jnp.cos(angles)[:, None, :]
    sine = jnp.sin(angles)[:, None, :]
    first_half = values[..., :half]
    second_half = values[..., half:]
    return jnp.concatenate(
        [first_half * cosine - second_half * sine, second_half * cosine + first_half * sine], -1
    )


def rms_normed(hidden_in, norm_gain):
    widened = hidden_in.astype(jnp.float32)
    factor = lax.rsqrt(jnp.mean(widened * widened, -1, keepdims=True) + 1e-05)
    return (widened, (widened * factor * norm_gain).astype(jnp.bfloat16))


def shards(hidden_in, norm_gain, wqkv_old, wo, key_cache, value_cache, lengths, section_order):
    tp_count = lax.axis_size("tp")
    section_count = tp_count // 4
    per_section = ROW_BLOCKS // section_count
    tp_index = lax.axis_index("tp")
    sub_index = lax.axis_index("sub")
    own_section = tp_index // 4
    device_rank = tp_index * 2 + sub_index
    cols_dev = wqkv_old.shape[2] // section_count
    rows_old = wqkv_old.shape[3]
    block_rows = rows_old // per_section
    old_block = wqkv_old[0, 0].reshape(section_count, cols_dev, rows_old)
    slot_ids = jnp.arange(section_count, dtype=jnp.int32)
    arrived = [lax.dynamic_index_in_dim(old_block, own_section, 0, keepdims=False)]
    for offset in range(1, section_count):
        outgoing = lax.dynamic_index_in_dim(
            old_block, (own_section + offset) % section_count, 0, keepdims=False
        )
        arrived.append(passed_along(outgoing, "tp", 4 * offset))
    received = jnp.stack(arrived, 0)
    sources = (own_section - slot_ids) % section_count
    block_ids = jnp.arange(ROW_BLOCKS, dtype=jnp.int32)
    local_source = (
        sources[:, None] * per_section + jnp.arange(per_section, dtype=jnp.int32)[None, :]
    ).reshape(ROW_BLOCKS)
    target_block = jnp.take(section_order, local_source, axis=0)
    placing = (target_block[None, :] == block_ids[:, None]).astype(jnp.bfloat16)
    received_blocks = jnp.transpose(
        received.reshape(section_count, cols_dev, per_section, block_rows), (0, 2, 1, 3)
    ).reshape(ROW_BLOCKS, cols_dev, block_rows)
    new_weight = jnp.einsum(
        "sa,acr->csr", placing, received_blocks, preferred_element_type=jnp.float32
    ).astype(jnp.bfloat16)
    new_weight = new_weight.reshape(cols_dev, ROW_BLOCKS * block_rows)
    widened, normed = rms_normed(hidden_in, norm_gain)
    projected = lax.dot_general(
        normed, new_weight, (((1,), (1,)), ((), ())), preferred_element_type=jnp.float32
    ).astype(jnp.bfloat16)
    gathered = lax.all_gather(projected[:, None, :], ("tp", "sub"), axis=1, tiled=True)
    seq_count = hidden_in.shape[0]
    projected_all = jnp.transpose(
        gathered.reshape(seq_count, section_count, RANKS, cols_dev), (0, 2, 1, 3)
    ).reshape(seq_count, -1)
    q_width = HEADS * HEAD_DIM
    kv_width = KV_HEADS * HEAD_DIM
    groups = HEADS // KV_HEADS
    queries = rotary(
        projected_all[:, :q_width].astype(jnp.float32).reshape(seq_count, HEADS, HEAD_DIM), lengths
    ).astype(jnp.bfloat16)
    new_keys = rotary(
        projected_all[:, q_width : q_width + kv_width]
        .astype(jnp.float32)
        .reshape(seq_count, KV_HEADS, HEAD_DIM),
        lengths,
    ).astype(jnp.bfloat16)
    new_values = (
        projected_all[:, q_width + kv_width :]
        .astype(jnp.float32)
        .reshape(seq_count, KV_HEADS, HEAD_DIM)
    )
    pos_count = key_cache.shape[1]
    positions = device_rank * pos_count + jnp.arange(pos_count, dtype=jnp.int32)
    usable = (positions[None, :] < lengths[:, None])[:, None, None, :]
    inverse = 1.0 / math.sqrt(HEAD_DIM)
    grouped = queries.reshape(seq_count, KV_HEADS, groups, HEAD_DIM)
    keys_local = key_cache.reshape(seq_count, pos_count, KV_HEADS, HEAD_DIM)
    values_local = value_cache.reshape(seq_count, pos_count, KV_HEADS, HEAD_DIM).astype(jnp.float32)
    scores = (
        jnp.einsum("bkgd,bpkd->bkgp", grouped, keys_local, preferred_element_type=jnp.float32)
        * inverse
    )
    local_top = jnp.max(jnp.where(usable, scores, -1e30), -1)
    weights = jnp.exp(jnp.where(usable, scores - local_top[..., None], -1e30))
    local_sum = jnp.sum(weights, -1).reshape(seq_count, HEADS)
    local_mix = jnp.einsum("bkgp,bpkd->bkgd", weights, values_local).reshape(
        seq_count, HEADS, HEAD_DIM
    )
    local_top = local_top.reshape(seq_count, HEADS)
    heads_dev = wo.shape[0] // HEAD_DIM
    first_head = device_rank * heads_dev
    tops_in, sums_in, mixes_in = (
        lax.all_to_all(local_top[None], ("tp", "sub"), split_axis=2, concat_axis=0, tiled=True),
        lax.all_to_all(local_sum[None], ("tp", "sub"), split_axis=2, concat_axis=0, tiled=True),
        lax.all_to_all(local_mix[None], ("tp", "sub"), split_axis=2, concat_axis=0, tiled=True),
    )
    best = jnp.max(tops_in, 0)
    factors = jnp.exp(tops_in - best[None])
    head_sum = jnp.sum(sums_in * factors, 0)
    head_mix = jnp.sum(mixes_in * factors[..., None], 0)
    own_queries = lax.dynamic_slice_in_dim(queries, first_head, heads_dev, 1).astype(jnp.float32)
    kv_index = (first_head + jnp.arange(heads_dev, dtype=jnp.int32)) // groups
    own_keys = jnp.take(new_keys, kv_index, axis=1).astype(jnp.float32)
    own_values = jnp.take(new_values, kv_index, axis=1)
    own_score = jnp.sum(own_queries * own_keys, -1) * inverse
    highest = jnp.maximum(best, own_score)
    old_scale = jnp.exp(best - highest)
    own_weight = jnp.exp(own_score - highest)
    numerator = head_mix * old_scale[..., None] + own_weight[..., None] * own_values
    denominator = head_sum * old_scale + own_weight
    attended = (
        (numerator / denominator[..., None])
        .reshape(seq_count, heads_dev * HEAD_DIM)
        .astype(jnp.bfloat16)
    )
    partial_out = jnp.dot(attended, wo, preferred_element_type=jnp.float32)
    summed_out = lax.psum(partial_out, ("tp", "sub"))
    mixed_out = (widened + summed_out).astype(jnp.bfloat16)
    return (mixed_out, new_weight[None, None])


def solution(mesh):
    placed = (
        P("replica", None),
        P("replica"),
        P(("replica", "tp"), "sub", None, None),
        P(("replica", "tp", "sub"), None),
        P("replica", ("tp", "sub"), None),
        P("replica", ("tp", "sub"), None),
        P("replica"),
        P("replica"),
    )
    return jax.shard_map(
        shards,
        mesh=mesh,
        in_specs=placed,
        out_specs=(P("replica", None), P(("replica", "tp"), "sub", None, None)),
        check_vma=False,
    )
```

profile of v0, /device:TPU:8, one launch (start us, length us, event | category | flops | bytes accessed | tf_op | source)
XLA Modules:
  0.0 444.4 jit_solution(11691780571699023312)
XLA Ops:
  7.2 9.9 %constant_dynamic-slice_fusion = (bf16[1,640,4096]{2,1,0:T(8,128)(2,1)}, bf16[640,4096]{1,0:T(8,128)(2,1)}) fusion(bf16[2,640,4096]{2,1,0:T(8,128)(2,1)} %bitcast.145, s32[]{:T(128)S(6)} %select_n.109, s32[]{:T(128)S(6)} %select_n.111), kind=kLoop, calls=%fused_computation.104 | loop fusion | bytes 20971528 | tf_op jit(solution)/shard_map/jit(dynamic_index_in_dim)/dynamic_slice | solution.py:52
  17.1 2.6 collective-permute-start
  19.9 8.3 %copy.49 = bf16[80,8,8,512]{3,2,1,0:T(8,128)(2,1)} copy(bf16[80,8,8,512]{3,1,2,0:T(8,128)(2,1)} %bitcast.144) | data formatting | bytes 10485760
  29.5 215.0 %collective-permute-done = bf16[640,4096]{1,0:T(8,128)(2,1)} collective-permute-done((bf16[640,4096]{1,0:T(8,128)(2,1)}, bf16[640,4096]{1,0:T(8,128)(2,1)}, u32[]{:S(2)}, u32[]{:S(2)}) %collective-permute-start) | collective-permute-done | bytes 5242912 | tf_op jit(solution)/shard_map/ppermute | solution.py:17
  244.5 6.1 %copy.50 = bf16[80,8,8,512]{3,2,1,0:T(8,128)(2,1)S(1)} copy(bf16[80,8,8,512]{3,1,2,0:T(8,128)(2,1)} %bitcast.49) | data formatting | bytes 10485760
  250.7 5.6 %fusion.3 = bf16[640,512,16]{1,2,0:T(8,128)(2,1)} fusion(bf16[1,640,8,512]{3,2,0,1:T(8,128)(2,1)S(1)} %bitcast.149, bf16[1,640,8,512]{3,2,0,1:T(8,128)(2,1)S(1)} %bitcast.148, s32[16]{0:T(128)S(1)} %and_select_fusion.2), kind=kOutput, calls=%fused_computation.7 | convolution fusion | flops 178258176 | bytes 20971584 | tf_op jit(solution)/shard_map/sa,acr->csr/dot_general | solution.py:69
  256.3 20.5 %copy.51 = bf16[80,8,16,512]{3,1,2,0:T(8,128)(2,1)} copy(bf16[80,8,16,512]{3,2,1,0:T(8,128)(2,1)} %bitcast.141) | data formatting | bytes 20971520
  276.8 6.8 %convolution_convert_fusion = bf16[4,640]{1,0:T(4,128)(2,1)S(1)} fusion(bf16[640,8192]{1,0:T(8,128)(2,1)} %bitcast.143, bf16[4,8192]{1,0:T(4,128)(2,1)S(1)} %copy-done.2, f32[8192]{0:T(1024)S(1)} %copy-done.3, f32[4]{0:T(128)S(1)} %add_rsqrt_fusion), kind=kOutput, calls=%fused_computation.17 | convolution fusion | flops 42076672 | bytes 10589200 | tf_op jit(solution)/shard_map/dot_general | solution.py:74
  283.6 19.8 %all-gather = bf16[4,10240]{1,0:T(4,128)(2,1)S(1)} all-gather(bf16[4,640]{1,0:T(4,128)(2,1)S(1)} %convolution_convert_fusion), channel_id=2, replica_groups=mesh['replica'=2,'tp'=8,'sub'=2] {'tp','sub'}, dimensions={1}, use_global_device_ids=true | all-gather | bytes 87040 | tf_op jit(solution)/shard_map/all_gather | solution.py:77
  303.8 0.8 select_reduce_fusion
  304.8 2.0 fusion.13
  306.8 0.7 copy.45
  307.6 6.6 %all-to-all-start.2 = ((f32[1,4,64]{1,0,2:T(1,128)}), f32[1,4,64]{1,0,2:T(1,128)S(1)}, u32[]{:S(2)}, u32[]{:S(2)}) async-start(f32[1,4,64]{1,0,2:T(1,128)} %bitcast.29), calls=%async_computation.2 | async-start | bytes 65536 | tf_op jit(solution)/shard_map/all_to_all | solution.py:121
  314.3 0.7 copy.37
  315.6 3.6 all-to-all-done.2
  319.3 5.0 %all-to-all-start.1 = ((f32[1,4,64]{1,0,2:T(1,128)}), f32[1,4,64]{1,0,2:T(1,128)S(1)}, u32[]{:S(2)}, u32[]{:S(2)}) async-start(f32[1,4,64]{1,0,2:T(1,128)} %bitcast.16), calls=%async_computation.1 | async-start | bytes 65536 | tf_op jit(solution)/shard_map/all_to_all | solution.py:120
  324.4 0.7 copy.36
  326.0 3.3 all-to-all-done.1
  329.4 5.0 %all-to-all-start = ((f32[1,4,64,128]{3,1,0,2:T(4,128)}), f32[1,4,64,128]{3,1,0,2:T(4,128)S(1)}, u32[]{:S(2)}, u32[]{:S(2)}) async-start(f32[1,4,64,128]{3,1,0,2:T(4,128)} %copy.36), calls=%async_computation | async-start | bytes 262144 | tf_op jit(solution)/shard_map/all_to_all | solution.py:122
  335.1 4.7 %all-to-all-done = f32[1,4,64,128]{3,1,0,2:T(4,128)S(1)} async-done(((f32[1,4,64,128]{3,1,0,2:T(4,128)}), f32[1,4,64,128]{3,1,0,2:T(4,128)S(1)}, u32[]{:S(2)}, u32[]{:S(2)}) %all-to-all-start) | async-done | bytes 131104 | tf_op jit(solution)/shard_map/all_to_all | solution.py:122
  339.9 5.3 %fusion.41 = f32[4,8192]{1,0:T(4,128)} fusion(bf16[512,8192]{1,0:T(8,128)(2,1)} %param.11, f32[1,4,4,128]{3,2,1,0:T(4,128)S(1)} %broadcast_bitcast_fusion, f32[4,4,128]{2,1,0:T(4,128)S(1)} %gather_fusion.2, f32[1,4,4,128]{3,2,1,0:T(4,128)S(1)} %broadcast_bitcast_fusion.1, f32[4,4,128]{2,0,1:T(4,128)S(1)} %multiply_reduce_fusion, f32[4,4]{0,1:T(4,128)S(1)} %copy.41, ...), kind=kOutput, calls=%fused_computation.69 | convolution fusion | flops 33566720 | bytes 8553024 | tf_op jit(solution)/shard_map/dot_general | solution.py:143
  345.2 16.5 %broadcast_in_dim_reshape.15 = bf16[1,1,640,8192]{3,2,1,0:T(8,128)(2,1)} reshape(bf16[640,16,512]{2,1,0:T(8,128)(2,1)} %bitcast.142) | data formatting | bytes 20971520 | tf_op jit(solution)/shard_map/broadcast_in_dim;reshape | solution.py:146
  361.7 74.2 %all-reduce.2.cloned.1.call-done = f32[4,8192]{1,0:T(4,128)} async-done(((f32[4,8192]{1,0:T(4,128)}), f32[4,8192]{1,0:T(4,128)}) %all-reduce.2.cloned.1.call-update) | async-done | bytes 131088 | tf_op jit(solution)/shard_map/psum | solution.py:144
  435.9 1.6 fusion.20
  (60 shorter events, 4.7 us)
Async XLA Ops:
  7.2 296.6 %copy-start = (bf16[4,256,1024]{2,1,0:T(8,128)(2,1)S(1)}, bf16[4,256,1024]{2,1,0:T(8,128)(2,1)}, u32[]{:S(2)}) copy-start(bf16[4,256,1024]{2,1,0:T(8,128)(2,1)} %param.12) | copy-start | bytes 6291460
  17.1 227.4 %collective-permute-start = (bf16[640,4096]{1,0:T(8,128)(2,1)}, bf16[640,4096]{1,0:T(8,128)(2,1)}, u32[]{:S(2)}, u32[]{:S(2)}) collective-permute-start(bf16[640,4096]{1,0:T(8,128)(2,1)} %get-tuple-element.8), channel_id=1, source_target_pairs={{0,8},{2,10},{4,12},{6,14},{8,0},{10,2},{12,4},{14,6},{1,9},{3,11}... | collective-permute-start | bytes 15728648 | tf_op jit(solution)/shard_map/ppermute | solution.py:17
  19.9 8.4 %copy-start.4 = (s32[4]{0:T(128)S(1)}, s32[4]{0:T(128)}, u32[]{:S(2)}) copy-start(s32[4]{0:T(128)} %param.14) | copy-start | bytes 52
  19.9 8.4 %copy-start.1 = (s32[16]{0:T(128)S(1)}, s32[16]{0:T(128)}, u32[]{:S(2)}) copy-start(s32[16]{0:T(128)} %param.15) | copy-start | bytes 196
  19.9 9.1 %copy-start.2 = (bf16[4,8192]{1,0:T(4,128)(2,1)S(1)}, bf16[4,8192]{1,0:T(4,128)(2,1)}, u32[]{:S(2)}) copy-start(bf16[4,8192]{1,0:T(4,128)(2,1)} %param.8) | copy-start | bytes 196612
  28.3 222.4 %slice-start = ((s8[5242880]{0:T(1024)(128)(4,1)}), s8[1048576]{0:T(1024)(128)(4,1)S(1)}, s32[]{:S(2)}) async-start(s8[5242880]{0:T(1024)(128)(4,1)} %bitcast.146), calls=%async_computation.4 | async-start | bytes 2097152
  244.5 6.1 %slice-start.1 = ((s8[5242880]{0:T(1024)(128)(4,1)}), s8[4194304]{0:T(1024)(128)(4,1)S(1)}, s32[]{:S(2)}) async-start(s8[5242880]{0:T(1024)(128)(4,1)} %bitcast.146), calls=%async_computation.5 | async-start | bytes 8388608
  256.3 20.6 %copy-start.3 = (f32[8192]{0:T(1024)S(1)}, f32[8192]{0:T(1024)}, u32[]{:S(2)}) copy-start(f32[8192]{0:T(1024)} %param.9) | copy-start | bytes 98308
  307.6 11.7 %all-to-all-start.2 = ((f32[1,4,64]{1,0,2:T(1,128)}), f32[1,4,64]{1,0,2:T(1,128)S(1)}, u32[]{:S(2)}, u32[]{:S(2)}) async-start(f32[1,4,64]{1,0,2:T(1,128)} %bitcast.29), calls=%async_computation.2 | async-start | bytes 65536 | tf_op jit(solution)/shard_map/all_to_all | solution.py:121
  319.3 10.1 %all-to-all-start.1 = ((f32[1,4,64]{1,0,2:T(1,128)}), f32[1,4,64]{1,0,2:T(1,128)S(1)}, u32[]{:S(2)}, u32[]{:S(2)}) async-start(f32[1,4,64]{1,0,2:T(1,128)} %bitcast.16), calls=%async_computation.1 | async-start | bytes 65536 | tf_op jit(solution)/shard_map/all_to_all | solution.py:120
  329.4 10.4 %all-to-all-start = ((f32[1,4,64,128]{3,1,0,2:T(4,128)}), f32[1,4,64,128]{3,1,0,2:T(4,128)S(1)}, u32[]{:S(2)}, u32[]{:S(2)}) async-start(f32[1,4,64,128]{3,1,0,2:T(4,128)} %copy.36), calls=%async_computation | async-start | bytes 262144 | tf_op jit(solution)/shard_map/all_to_all | solution.py:122
  334.4 101.6 %all-reduce.2.cloned.1.call-start = ((), (), s32[]{:S(2)}) async-start(), calls=%async_computation.3 | async-start | bytes 262144 | tf_op jit(solution)/shard_map/psum | solution.py:144
Sparse Core Ops, SparseCore 0:
  345.4 90.5 all-reduce.1
where the time goes:
time: 445 us; the launch traced here: 444 us
  waiting for transfers between devices  301 us (68%)
  local copies, waits for them, and re-layouts  66.7 us (15%)
  matrix products  20.4 us (5%)
  blocking collectives  19.8 us (4%)
  starting transfers between devices  19.2 us (4%)
  between operations  14.3 us (3%)
    ppermute x1, waiting for transfers between devices, passed_along(): return lax.ppermute(value, axis, pairs)  215 us
    psum x1, waiting for transfers between devices, shards(): summed_out = lax.psum(partial_out, ('tp', 'sub'))  74.2 us
    unnamed x20, local copies, waits for them, and re-layouts  35.2 us
    all_gather x1, blocking collectives, shards(): lax.all_gather(projected[:, None, :], ('tp', 'sub'), axis=1, tiled=True)  19.8 us
    another operation x1, local copies, waits for them, and re-layouts, shards(): return (mixed_out, new_weight[None, None])  16.5 us
    dynamic_slice x1, local copies, waits for them, and re-layouts, shards(): lax.dynamic_index_in_dim(old_block, own_section, 0, keepdims=False)  9.85 us
  transfers between devices with their start and end apart: 5, of which 5 were waited for; matrix products, arithmetic and copies ran while one was open for 7% of the time, Pallas kernels for 0%

commit v1 on v0

--- a/solution.py
+++ b/solution.py
@@ -141,7 +141,7 @@
         .astype(jnp.bfloat16)
     )
     partial_out = jnp.dot(attended, wo, preferred_element_type=jnp.float32)
-    summed_out = lax.psum(partial_out, ("tp", "sub"))
+    summed_out = jnp.sum(lax.all_gather(partial_out, ("tp", "sub")), axis=0)
     mixed_out = (widened + summed_out).astype(jnp.bfloat16)
     return (mixed_out, new_weight[None, None])
 

time: 445 us -> 399 us (0.90)
  waiting for transfers between devices: 301 us -> 250 us
    psum x1 -> x0, waiting for transfers between devices: 74.2 us -> none  [shards(): summed_out = lax.psum(partial_out, ('tp', 'sub'))]
    all_gather x0 -> x1, waiting for transfers between devices: none -> 23.7 us  [shards(): summed_out = jnp.sum(lax.all_gather(partial_out, ('tp', 'sub')), axis=0)]
  transfers between devices with their start and end apart: 5 -> 5, of which waited for: 5 -> 5; matrix products, arithmetic and copies ran while one was open for 7% -> 8% of each run, Pallas kernels for 0% -> 0%
where the time goes in v1:
time: 399 us; the launch traced here: 395 us
  waiting for transfers between devices  250 us (63%)
  local copies, waits for them, and re-layouts  66.8 us (17%)
  matrix products  20.4 us (5%)
  blocking collectives  19.8 us (5%)
  starting transfers between devices  19.2 us (5%)
  between operations  14.3 us (4%)
  other arithmetic  4.04 us (1%)
    ppermute x1, waiting for transfers between devices, passed_along(): return lax.ppermute(value, axis, pairs)  215 us
    unnamed x20, local copies, waits for them, and re-layouts  35.2 us
    all_gather x1, waiting for transfers between devices, shards(): summed_out = jnp.sum(lax.all_gather(partial_out, ('tp', 'sub')), axis=0)  23.7 us
    all_gather x1, blocking collectives, shards(): lax.all_gather(projected[:, None, :], ('tp', 'sub'), axis=1, tiled=True)  19.8 us
    another operation x1, local copies, waits for them, and re-layouts, shards(): return (mixed_out, new_weight[None, None])  16.5 us
    dynamic_slice x1, local copies, waits for them, and re-layouts, shards(): lax.dynamic_index_in_dim(old_block, own_section, 0, keepdims=False)  9.85 us
  transfers between devices with their start and end apart: 5, of which 5 were waited for; matrix products, arithmetic and copies ran while one was open for 8% of the time, Pallas kernels for 0%

profile of v1, /device:TPU:8, one launch (start us, length us, event | category | flops | bytes accessed | tf_op | source)
XLA Modules:
  0.0 394.9 jit_solution(15745159634802425812)
XLA Ops:
  7.2 9.9 %constant_dynamic-slice_fusion = (bf16[1,640,4096]{2,1,0:T(8,128)(2,1)}, bf16[640,4096]{1,0:T(8,128)(2,1)}) fusion(bf16[2,640,4096]{2,1,0:T(8,128)(2,1)} %bitcast.147, s32[]{:T(128)S(6)} %select_n.109, s32[]{:T(128)S(6)} %select_n.111), kind=kLoop, calls=%fused_computation.104 | loop fusion | bytes 20971528 | tf_op jit(solution)/shard_map/jit(dynamic_index_in_dim)/dynamic_slice | solution.py:52
  17.1 2.6 collective-permute-start
  19.9 8.3 %copy.49 = bf16[80,8,8,512]{3,2,1,0:T(8,128)(2,1)} copy(bf16[80,8,8,512]{3,1,2,0:T(8,128)(2,1)} %bitcast.146) | data formatting | bytes 10485760
  29.5 215.0 %collective-permute-done = bf16[640,4096]{1,0:T(8,128)(2,1)} collective-permute-done((bf16[640,4096]{1,0:T(8,128)(2,1)}, bf16[640,4096]{1,0:T(8,128)(2,1)}, u32[]{:S(2)}, u32[]{:S(2)}) %collective-permute-start) | collective-permute-done | bytes 5242912 | tf_op jit(solution)/shard_map/ppermute | solution.py:17
  244.5 6.1 %copy.50 = bf16[80,8,8,512]{3,2,1,0:T(8,128)(2,1)S(1)} copy(bf16[80,8,8,512]{3,1,2,0:T(8,128)(2,1)} %bitcast.50) | data formatting | bytes 10485760
  250.7 5.6 %fusion.3 = bf16[640,512,16]{1,2,0:T(8,128)(2,1)} fusion(bf16[1,640,8,512]{3,2,0,1:T(8,128)(2,1)S(1)} %bitcast.151, bf16[1,640,8,512]{3,2,0,1:T(8,128)(2,1)S(1)} %bitcast.150, s32[16]{0:T(128)S(1)} %and_select_fusion.2), kind=kOutput, calls=%fused_computation.8 | convolution fusion | flops 178258176 | bytes 20971584 | tf_op jit(solution)/shard_map/sa,acr->csr/dot_general | solution.py:69
  256.3 20.5 %copy.51 = bf16[80,8,16,512]{3,1,2,0:T(8,128)(2,1)} copy(bf16[80,8,16,512]{3,2,1,0:T(8,128)(2,1)} %bitcast.143) | data formatting | bytes 20971520
  276.8 6.8 %convolution_convert_fusion = bf16[4,640]{1,0:T(4,128)(2,1)S(1)} fusion(bf16[640,8192]{1,0:T(8,128)(2,1)} %bitcast.145, bf16[4,8192]{1,0:T(4,128)(2,1)S(1)} %copy-done.2, f32[8192]{0:T(1024)S(1)} %copy-done.3, f32[4]{0:T(128)S(1)} %add_rsqrt_fusion), kind=kOutput, calls=%fused_computation.18 | convolution fusion | flops 42076672 | bytes 10589200 | tf_op jit(solution)/shard_map/dot_general | solution.py:74
  283.6 19.8 %all-gather = bf16[4,10240]{1,0:T(4,128)(2,1)S(1)} all-gather(bf16[4,640]{1,0:T(4,128)(2,1)S(1)} %convolution_convert_fusion), channel_id=2, replica_groups=mesh['replica'=2,'tp'=8,'sub'=2] {'tp','sub'}, dimensions={1}, use_global_device_ids=true | all-gather | bytes 87040 | tf_op jit(solution)/shard_map/all_gather | solution.py:77
  303.8 0.8 select_reduce_fusion
  304.8 2.0 fusion.13
  306.8 0.7 copy.45
  307.6 6.6 %all-to-all-start.2 = ((f32[1,4,64]{1,0,2:T(1,128)}), f32[1,4,64]{1,0,2:T(1,128)S(1)}, u32[]{:S(2)}, u32[]{:S(2)}) async-start(f32[1,4,64]{1,0,2:T(1,128)} %bitcast.29), calls=%async_computation.2 | async-start | bytes 65536 | tf_op jit(solution)/shard_map/all_to_all | solution.py:121
  314.3 0.7 copy.37
  315.6 3.6 all-to-all-done.2
  319.3 5.0 %all-to-all-start.1 = ((f32[1,4,64]{1,0,2:T(1,128)}), f32[1,4,64]{1,0,2:T(1,128)S(1)}, u32[]{:S(2)}, u32[]{:S(2)}) async-start(f32[1,4,64]{1,0,2:T(1,128)} %bitcast.16), calls=%async_computation.1 | async-start | bytes 65536 | tf_op jit(solution)/shard_map/all_to_all | solution.py:120
  324.4 0.7 copy.36
  326.0 3.3 all-to-all-done.1
  329.4 5.0 %all-to-all-start = ((f32[1,4,64,128]{3,1,0,2:T(4,128)}), f32[1,4,64,128]{3,1,0,2:T(4,128)S(1)}, u32[]{:S(2)}, u32[]{:S(2)}) async-start(f32[1,4,64,128]{3,1,0,2:T(4,128)} %copy.36), calls=%async_computation | async-start | bytes 262144 | tf_op jit(solution)/shard_map/all_to_all | solution.py:122
  335.1 4.6 %all-to-all-done = f32[1,4,64,128]{3,1,0,2:T(4,128)S(1)} async-done(((f32[1,4,64,128]{3,1,0,2:T(4,128)}), f32[1,4,64,128]{3,1,0,2:T(4,128)S(1)}, u32[]{:S(2)}, u32[]{:S(2)}) %all-to-all-start) | async-done | bytes 131104 | tf_op jit(solution)/shard_map/all_to_all | solution.py:122
  339.9 5.3 %convolution_bitcast_fusion = f32[1,4,8192]{2,1,0:T(4,128)} fusion(bf16[512,8192]{1,0:T(8,128)(2,1)} %param.11, f32[1,4,4,128]{3,2,1,0:T(4,128)S(1)} %broadcast_bitcast_fusion, f32[4,4,128]{2,1,0:T(4,128)S(1)} %gather_fusion.2, f32[1,4,4,128]{3,2,1,0:T(4,128)S(1)} %broadcast_bitcast_fusion.1, f32[4,4,128]{2,0,1:T(4,128)S(1)} %multiply_reduce_fusion, ...), kind=kOutput, calls=%fused_computation.7 | convolution fusion | flops 33566720 | bytes 8553024 | tf_op jit(solution)/shard_map/dot_general | solution.py:143
  345.2 16.5 %broadcast_in_dim_reshape.15 = bf16[1,1,640,8192]{3,2,1,0:T(8,128)(2,1)} reshape(bf16[640,16,512]{2,1,0:T(8,128)(2,1)} %bitcast.144) | data formatting | bytes 20971520 | tf_op jit(solution)/shard_map/broadcast_in_dim;reshape | solution.py:146
  361.8 23.7 %all-gather.5.cloned.1.call-done = f32[16,4,8192]{2,1,0:T(4,128)} async-done(((f32[1,4,8192]{2,1,0:T(4,128)}), f32[16,4,8192]{2,1,0:T(4,128)}) %all-gather.5.cloned.1.call-update) | async-done | bytes 2097168 | tf_op jit(solution)/shard_map/all_gather | solution.py:144
  385.5 1.9 reduce_sum.59
  (61 shorter events, 5.3 us)
Async XLA Ops:
  7.2 296.6 %copy-start = (bf16[4,256,1024]{2,1,0:T(8,128)(2,1)S(1)}, bf16[4,256,1024]{2,1,0:T(8,128)(2,1)}, u32[]{:S(2)}) copy-start(bf16[4,256,1024]{2,1,0:T(8,128)(2,1)} %param.12) | copy-start | bytes 6291460
  17.1 227.4 %collective-permute-start = (bf16[640,4096]{1,0:T(8,128)(2,1)}, bf16[640,4096]{1,0:T(8,128)(2,1)}, u32[]{:S(2)}, u32[]{:S(2)}) collective-permute-start(bf16[640,4096]{1,0:T(8,128)(2,1)} %get-tuple-element.8), channel_id=1, source_target_pairs={{0,8},{2,10},{4,12},{6,14},{8,0},{10,2},{12,4},{14,6},{1,9},{3,11}... | collective-permute-start | bytes 15728648 | tf_op jit(solution)/shard_map/ppermute | solution.py:17
  19.9 8.4 %copy-start.4 = (s32[4]{0:T(128)S(1)}, s32[4]{0:T(128)}, u32[]{:S(2)}) copy-start(s32[4]{0:T(128)} %param.14) | copy-start | bytes 52
  19.9 8.4 %copy-start.1 = (s32[16]{0:T(128)S(1)}, s32[16]{0:T(128)}, u32[]{:S(2)}) copy-start(s32[16]{0:T(128)} %param.15) | copy-start | bytes 196
  19.9 9.1 %copy-start.2 = (bf16[4,8192]{1,0:T(4,128)(2,1)S(1)}, bf16[4,8192]{1,0:T(4,128)(2,1)}, u32[]{:S(2)}) copy-start(bf16[4,8192]{1,0:T(4,128)(2,1)} %param.8) | copy-start | bytes 196612
  28.3 222.4 %slice-start = ((s8[5242880]{0:T(1024)(128)(4,1)}), s8[1048576]{0:T(1024)(128)(4,1)S(1)}, s32[]{:S(2)}) async-start(s8[5242880]{0:T(1024)(128)(4,1)} %bitcast.148), calls=%async_computation.4 | async-start | bytes 2097152
  244.5 6.1 %slice-start.1 = ((s8[5242880]{0:T(1024)(128)(4,1)}), s8[4194304]{0:T(1024)(128)(4,1)S(1)}, s32[]{:S(2)}) async-start(s8[5242880]{0:T(1024)(128)(4,1)} %bitcast.148), calls=%async_computation.5 | async-start | bytes 8388608
  256.3 20.6 %copy-start.3 = (f32[8192]{0:T(1024)S(1)}, f32[8192]{0:T(1024)}, u32[]{:S(2)}) copy-start(f32[8192]{0:T(1024)} %param.9) | copy-start | bytes 98308
  307.6 11.7 %all-to-all-start.2 = ((f32[1,4,64]{1,0,2:T(1,128)}), f32[1,4,64]{1,0,2:T(1,128)S(1)}, u32[]{:S(2)}, u32[]{:S(2)}) async-start(f32[1,4,64]{1,0,2:T(1,128)} %bitcast.29), calls=%async_computation.2 | async-start | bytes 65536 | tf_op jit(solution)/shard_map/all_to_all | solution.py:121
  319.3 10.1 %all-to-all-start.1 = ((f32[1,4,64]{1,0,2:T(1,128)}), f32[1,4,64]{1,0,2:T(1,128)S(1)}, u32[]{:S(2)}, u32[]{:S(2)}) async-start(f32[1,4,64]{1,0,2:T(1,128)} %bitcast.16), calls=%async_computation.1 | async-start | bytes 65536 | tf_op jit(solution)/shard_map/all_to_all | solution.py:120
  329.4 10.4 %all-to-all-start = ((f32[1,4,64,128]{3,1,0,2:T(4,128)}), f32[1,4,64,128]{3,1,0,2:T(4,128)S(1)}, u32[]{:S(2)}, u32[]{:S(2)}) async-start(f32[1,4,64,128]{3,1,0,2:T(4,128)} %copy.36), calls=%async_computation | async-start | bytes 262144 | tf_op jit(solution)/shard_map/all_to_all | solution.py:122
  334.4 51.1 %all-gather.5.cloned.1.call-start = ((), (), s32[]{:S(2)}) async-start(), calls=%async_computation.3 | async-start | bytes 2228224 | tf_op jit(solution)/shard_map/all_gather | solution.py:144
Sparse Core Ops, SparseCore 0:
  345.3 40.0 all-gather.4
